TPU v7x, 32 devices: a whole 2x2x4 slice. The times are simulated.
32 devices in a mesh: row: 4 (over z), col: 8 (over y, x, core).
Axes of the slice: x: 2, y: 2, z: 4, core: 2. Of those that a mesh axis runs over, the one named last changes fastest.
Arguments:
- fine_residual: bfloat16 [16, 524288], P(None, ('row', 'col')), may hold values from -6 to 6
- tiles_one: bfloat16 [8192, 128, 128], P(('row', 'col')), may hold values from -0.1875 to 0.1875
- pointers_one: int32 [4128], P(('row', 'col')), may hold values from 0 to 256, as said below
- columns_one: int32 [8192], P(('row', 'col')), may hold values from 0 to 1023, as said below
- points_one: int32 [131072], P(('col', 'row')), may hold values from 0 to 16383, as said below
- tiles_two: bfloat16 [4096, 128, 128], P(('row', 'col')), may hold values from -0.125 to 0.125
- pointers_two: int32 [2080], P(('row', 'col')), may hold values from 0 to 128, as said below
- columns_two: int32 [4096], P(('row', 'col')), may hold values from 0 to 127
- points_two: int32 [32768], P(('row', 'col')), may hold values from 0 to 4095, as said below
- tiles_three: bfloat16 [512, 128, 128], P(('row', 'col')), may hold values from -0.1875 to 0.1875
- pointers_three: int32 [288], P(('row', 'col')), may hold values from 0 to 16, as said below
- columns_three: int32 [512], P(('row', 'col')), may hold values from 0 to 63
- points_three: int32 [8192], P(('col', 'row')), may hold values from 0 to 1023, as said below
Outputs:
- coarse_one: bfloat16 [16, 131072], P(None, ('col', 'row'))
- coarse_two: bfloat16 [16, 32768], P(None, ('row', 'col'))
- coarse_three: bfloat16 [16, 8192], P(None, ('col', 'row'))
Inputs may be any that keep to these rules, and one draw needn't show every extreme that they name: `pointers_one`: each tile set's 128 + 1 pointers start at 0 and never fall; the last is that set's live slot count, at most 256; some set has 256 live slots. `pointers_two`: each tile set's 64 + 1 pointers start at 0 and never fall; the last is that set's live slot count, at most 128; some set has 128 live slots. `pointers_three`: each tile set's 8 + 1 pointers start at 0 and never fall; the last is that set's live slot count, at most 16; some set has 16 live slots. `columns_one`: among the live slots of one tile set, at most 32 name block columns with the same quotient by 128; some set reaches 32. `points_one`: values are distinct within each aligned run of 4096 entries. `points_two`: values are distinct within each aligned run of 1024 entries. `points_three`: values are distinct within each aligned run of 256 entries.
All inputs are finite; a program needn't handle non-finite values.
Results may differ from a plain program's by a relative error of at most 0.0057.
Values may be sent and summed in bfloat16 or wider, within the bound.
No kernel may reach another device: no remote copies, remote signals or barrier semaphores. Data moves between devices by JAX's collectives and lax.ppermute only.
A program may use at most 128 MiB of HBM per device.

v0:
```python
import jax
import jax.numpy as jnp
from jax import lax
from jax.sharding import PartitionSpec as P


def slot_layout(pointers, slot_count):
    block_count = pointers.shape[0] - 1
    positions = jnp.arange(slot_count, dtype=jnp.int32)
    is_live = positions < pointers[block_count]
    finished = jnp.sum((pointers[1:][None, :] <= positions[:, None]).astype(jnp.int32), axis=1)
    segment = jnp.where(is_live, finished, block_count)
    return (is_live, segment)


def block_sums(products, segment, block_count):
    summed = jax.ops.segment_sum(
        products, segment, num_segments=block_count + 1, indices_are_sorted=True
    )
    summed = summed[:block_count]
    return jnp.transpose(summed, (1, 0, 2)).reshape(summed.shape[1], block_count * summed.shape[2])


def group_products(tiles, fine_group, columns, segment, block_count):
    vector_count = fine_group.shape[0]
    tile_edge = tiles.shape[1]
    blocks = fine_group.reshape(vector_count, fine_group.shape[1] // tile_edge, tile_edge)
    picked = jnp.take(blocks, columns, axis=1)
    products = jnp.einsum("sij,vsj->svi", tiles, picked, preferred_element_type=jnp.float32)
    return block_sums(products, segment, block_count)


def add_points(partial_value, own_piece, points, position):
    injected = jnp.take(own_piece, points, axis=1).astype(jnp.float32)
    offset = position * points.shape[0]
    current = lax.dynamic_slice_in_dim(partial_value, offset, points.shape[0], 1)
    return lax.dynamic_update_slice_in_dim(partial_value, current + injected, offset, 1)


def on_device(
    fine_residual,
    tiles_one,
    pointers_one,
    columns_one,
    points_one,
    tiles_two,
    pointers_two,
    columns_two,
    points_two,
    tiles_three,
    pointers_three,
    columns_three,
    points_three,
):
    tile_edge = tiles_one.shape[1]
    vector_count = fine_residual.shape[0]
    slots_first = tiles_one.shape[0]
    blocks_first = pointers_one.shape[0] - 1
    live_first, segment_first = slot_layout(pointers_one, slots_first)
    peer_count = lax.axis_size("col")
    per_peer = slots_first // peer_count
    blocks_peer = fine_residual.shape[1] // tile_edge
    owner_peer = columns_one // blocks_peer
    within = columns_one % blocks_peer
    peer_ids = jnp.arange(peer_count, dtype=jnp.int32)
    peer_hits = ((owner_peer[:, None] == peer_ids[None, :]) & live_first[:, None]).astype(jnp.int32)
    peer_rank = jnp.sum(jnp.cumsum(peer_hits, axis=0) * peer_hits, axis=1) - 1
    target = jnp.where(live_first, owner_peer * per_peer + peer_rank, peer_count * per_peer)
    requests = jnp.zeros((peer_count * per_peer,), jnp.int32).at[target].set(within, mode="drop")
    requests = requests.reshape(peer_count, per_peer)
    own_blocks = jnp.transpose(
        fine_residual.reshape(vector_count, blocks_peer, tile_edge), (1, 0, 2)
    )
    found_blocks = jnp.take(
        own_blocks, lax.all_to_all(requests, "col", split_axis=0, concat_axis=0, tiled=True), axis=0
    )
    replies = lax.all_to_all(found_blocks, "col", split_axis=0, concat_axis=0, tiled=True)
    flat_replies = replies.reshape(peer_count * per_peer, vector_count, tile_edge)
    picked = jnp.take(flat_replies, jnp.minimum(target, peer_count * per_peer - 1), axis=0)
    products = jnp.einsum("sij,svj->svi", tiles_one, picked, preferred_element_type=jnp.float32)
    partial_one = block_sums(products, segment_first, blocks_first)
    partial_one = add_points(partial_one, fine_residual, points_one, lax.axis_index("row"))
    coarse_one = lax.psum_scatter(partial_one, "row", scatter_dimension=1, tiled=True).astype(
        jnp.bfloat16
    )
    group_one = lax.all_gather(coarse_one, "row", axis=1, tiled=True)
    segment_second = slot_layout(pointers_two, tiles_two.shape[0])[1]
    partial_two = group_products(
        tiles_two, group_one, columns_two, segment_second, pointers_two.shape[0] - 1
    )
    partial_two = add_points(partial_two, coarse_one, points_two, lax.axis_index("col"))
    coarse_two = lax.psum_scatter(partial_two, "col", scatter_dimension=1, tiled=True).astype(
        jnp.bfloat16
    )
    group_two = lax.all_gather(coarse_two, "col", axis=1, tiled=True)
    segment_third = slot_layout(pointers_three, tiles_three.shape[0])[1]
    partial_three = group_products(
        tiles_three, group_two, columns_three, segment_third, pointers_three.shape[0] - 1
    )
    partial_three = add_points(partial_three, coarse_two, points_three, lax.axis_index("row"))
    coarse_three = lax.psum_scatter(partial_three, "row", scatter_dimension=1, tiled=True).astype(
        jnp.bfloat16
    )
    return (coarse_one, coarse_two, coarse_three)


def solution(mesh):
    placed = (
        P(None, ("row", "col")),
        P(("row", "col"), None, None),
        P(("row", "col")),
        P(("row", "col")),
        P(("col", "row")),
        P(("row", "col"), None, None),
        P(("row", "col")),
        P(("row", "col")),
        P(("row", "col")),
        P(("row", "col"), None, None),
        P(("row", "col")),
        P(("row", "col")),
        P(("col", "row")),
    )
    return jax.shard_map(
        on_device,
        mesh=mesh,
        in_specs=placed,
        out_specs=(P(None, ("col", "row")), P(None, ("row", "col")), P(None, ("col", "row"))),
        check_vma=False,
    )
```

profile of v0, /device:TPU:0, one launch (start us, length us, event | category | flops | bytes accessed | tf_op | source)
XLA Modules:
  0.0 434.2 jit_solution(3455119433022537755)
XLA Ops:
  12.1 1.4 scatter_custom_fusion
  14.2 5.2 %all-to-all-start = ((s32[8,1,32]{2,1,0:T(1,128)}), s32[8,1,32]{2,1,0:T(1,128)S(1)}, u32[]{:S(2)}, u32[]{:S(2)}) async-start(s32[8,1,32]{2,1,0:T(1,128)} %all_to_all.13), calls=%async_computation | async-start | bytes 8192 | tf_op jit(solution)/shard_map/all_to_all | solution.py:75
  20.5 3.5 all-to-all-done
  26.2 3.6 all-to-all-start.1
  29.9 3.1 copy.76
  33.0 16.9 %gather_fusion.2 = bf16[4096,16]{1,0:T(8,128)(2,1)} fusion(bf16[16,16384]{0,1:T(8,128)(2,1)} %copy.76, s32[4096]{0:T(1024)S(1)} %fusion.16), kind=kCustom, calls=%fused_computation.2 | custom fusion | bytes 278528 | tf_op jit(solution)/shard_map/jit(_take)/gather | solution.py:34
  52.3 9.3 %fusion.1 = f32[256,16,128]{2,1,0:T(8,128)} fusion(bf16[256,128,128]{2,1,0:T(8,128)(2,1)} %param.14, bf16[256,16,128]{2,1,0:T(8,128)(2,1)S(1)} %gather_fusion.1, pred[256]{0:T(512)(128)(4,1)S(1)} %get-tuple-element.21), kind=kOutput, calls=%fused_computation.14 | convolution fusion | flops 134742016 | bytes 11534592 | tf_op jit(solution)/shard_map/sij,svj->svi/dot_general | solution.py:80
  61.6 20.6 %scatter_fusion = f32[129,16,128]{2,1,0:T(8,128)S(1)} fusion(f32[129,16,128]{2,1,0:T(8,128)S(1)} %broadcast_in_dim.121, s32[256]{0:T(256)S(1)} %bitcast.75, f32[256,16,128]{2,1,0:T(8,128)} %fusion.1), kind=kCustom, calls=%fused_computation.8 | custom fusion | flops 524288 | bytes 6292480 | tf_op jit(solution)/shard_map/scatter-add | solution.py:17
  82.3 4.6 %copy.94 = f32[16,128,128]{0,2,1:T(8,128)} copy(f32[16,128,128]{2,0,1:T(8,128)S(1)} %slice_bitcast_fusion) | data formatting | bytes 2097152 | tf_op jit(solution)/shard_map/reshape | solution.py:21
  87.0 3.0 fusion
  92.1 144.5 %reduce-scatter.4.cloned.1.call-done = f32[16,4096]{0,1:T(8,128)} async-done(((f32[16,16384]{0,1:T(8,128)}), f32[16,4096]{0,1:T(8,128)}) %reduce-scatter.4.cloned.1.call-update) | async-done | bytes 262160 | tf_op jit(solution)/shard_map/reduce_scatter | solution.py:83
  236.6 1.7 convert_element_type.35
  238.3 72.1 %all_gather.6 = bf16[16,16384]{0,1:T(8,128)(2,1)} all-gather(bf16[16,4096]{0,1:T(8,128)(2,1)S(1)} %convert_element_type.35), channel_id=1, replica_groups=mesh['row'=4,'col'=8] {'row'}, dimensions={1}, use_global_device_ids=true | all-gather | bytes 655360 | tf_op jit(solution)/shard_map/all_gather | solution.py:86
  310.4 3.5 copy.79
  314.6 4.5 %fusion.5 = f32[128,16,128]{2,1,0:T(8,128)S(1)} fusion(bf16[128,128,128]{2,1,0:T(8,128)(2,1)} %param.18, bf16[128,16,128]{2,1,0:T(8,128)(2,1)S(1)} %gather_fusion.3, pred[128]{0:T(512)(128)(4,1)S(1)} %compare_and_fusion.5), kind=kOutput, calls=%fused_computation.22 | convolution fusion | flops 67371008 | bytes 5767296 | tf_op jit(solution)/shard_map/sij,vsj->svi/dot_general | solution.py:29
  319.2 5.5 %scatter_fusion.1 = f32[65,16,128]{2,1,0:T(8,128)S(1)} fusion(f32[65,16,128]{2,1,0:T(8,128)S(1)} %broadcast_in_dim.133, s32[128]{0:T(128)S(1)} %fusion.22, f32[128,16,128]{2,1,0:T(8,128)S(1)} %fusion.5), kind=kCustom, calls=%fused_computation.9 | custom fusion | flops 262144 | bytes 3146240 | tf_op jit(solution)/shard_map/scatter-add | solution.py:17
  324.8 2.6 copy.96
  327.3 3.2 gather_fusion.4
  330.6 2.0 fusion.4
  334.1 50.5 %reduce-scatter.6.cloned.1.call-done = f32[16,1024]{0,1:T(8,128)} async-done(((f32[16,8192]{0,1:T(8,128)}), f32[16,1024]{0,1:T(8,128)}) %reduce-scatter.6.cloned.1.call-update) | async-done | bytes 65552 | tf_op jit(solution)/shard_map/reduce_scatter | solution.py:92
  385.7 15.3 %all_gather.7 = bf16[16,8192]{0,1:T(8,128)(2,1)} all-gather(bf16[16,1024]{0,1:T(8,128)(2,1)S(1)} %convert_element_type.38), channel_id=1, replica_groups=mesh['row'=4,'col'=8] {'col'}, dimensions={1}, use_global_device_ids=true | all-gather | bytes 294912 | tf_op jit(solution)/shard_map/all_gather | solution.py:95
  401.0 1.9 copy.84
  408.6 17.8 %reduce-scatter.8.cloned.1.call-done = f32[16,256]{1,0:T(8,128)} async-done(((f32[16,1024]{1,0:T(8,128)}), f32[16,256]{1,0:T(8,128)}) %reduce-scatter.8.cloned.1.call-update) | async-done | bytes 16400 | tf_op jit(solution)/shard_map/reduce_scatter | solution.py:101
  426.4 1.3 convert_element_type.41
  (96 shorter events, 22.5 us)
Async XLA Ops:
  7.2 396.3 %copy-start = (bf16[16,128,128]{2,1,0:T(8,128)(2,1)S(1)}, bf16[16,128,128]{2,1,0:T(8,128)(2,1)}, u32[]{:S(2)}) copy-start(bf16[16,128,128]{2,1,0:T(8,128)(2,1)} %param.22) | copy-start | bytes 1572868
  7.2 22.7 %copy-start.7 = (s32[129]{0:T(256)S(1)}, s32[129]{0:T(256)}, u32[]{:S(2)}) copy-start(s32[129]{0:T(256)} %param.15) | copy-start | bytes 1552
  7.2 22.8 %copy-start.1 = (bf16[16,16384]{1,0:T(8,128)(2,1)S(1)}, bf16[16,16384]{1,0:T(8,128)(2,1)}, u32[]{:S(2)}) copy-start(bf16[16,16384]{1,0:T(8,128)(2,1)} %param.13) | copy-start | bytes 1572868
  7.2 22.6 %copy-start.4 = (s32[4096]{0:T(1024)S(1)}, s32[4096]{0:T(1024)}, u32[]{:S(2)}) copy-start(s32[4096]{0:T(1024)} %param.17) | copy-start | bytes 49156
  14.2 9.8 %all-to-all-start = ((s32[8,1,32]{2,1,0:T(1,128)}), s32[8,1,32]{2,1,0:T(1,128)S(1)}, u32[]{:S(2)}, u32[]{:S(2)}) async-start(s32[8,1,32]{2,1,0:T(1,128)} %all_to_all.13), calls=%async_computation | async-start | bytes 8192 | tf_op jit(solution)/shard_map/all_to_all | solution.py:75
  26.2 25.2 %all-to-all-start.1 = ((bf16[8,32,16,128]{3,2,1,0:T(8,128)(2,1)}), bf16[8,32,16,128]{3,2,1,0:T(8,128)(2,1)S(1)}, u32[]{:S(2)}, u32[]{:S(2)}) async-start(bf16[8,32,16,128]{3,2,1,0:T(8,128)(2,1)} %broadcast_select_fusion), calls=%async_computation.1 | async-start | bytes 2097152 | tf_op jit(solution)/shard_map/all_to_all | solution.py:77
  29.8 206.8 %reduce-scatter.4.cloned.1.call-start = ((), (), s32[]{:S(2)}) async-start(), calls=%async_computation.5 | async-start | bytes 10485760 | tf_op jit(solution)/shard_map/reduce_scatter | solution.py:83
  82.3 4.6 %copy-start.2 = (bf16[4096,16]{1,0:T(8,128)(2,1)S(1)}, bf16[4096,16]{1,0:T(8,128)(2,1)}, u32[]{:S(2)}) copy-start(bf16[4096,16]{1,0:T(8,128)(2,1)} %gather_fusion.2) | copy-start | bytes 393220
  89.9 0.7 copy-start.8
  89.9 1.3 copy-start.9
  89.9 1.3 copy-start.11
  89.9 2.1 copy-start.6
  89.9 2.1 copy-start.5
  90.0 294.7 %reduce-scatter.6.cloned.1.call-start = ((), (), s32[]{:S(2)}) async-start(), calls=%async_computation.6 | async-start | bytes 4718592 | tf_op jit(solution)/shard_map/reduce_scatter | solution.py:92
  324.7 7.9 %copy-start.10 = (s32[9]{0:T(128)S(1)}, s32[9]{0:T(128)}, u32[]{:S(2)}) copy-start(s32[9]{0:T(128)} %param.23) | copy-start | bytes 112
  332.6 93.8 %reduce-scatter.8.cloned.1.call-start = ((), (), s32[]{:S(2)}) async-start(), calls=%async_computation.7 | async-start | bytes 81920 | tf_op jit(solution)/shard_map/reduce_scatter | solution.py:101
  406.2 0.6 copy-start.3
Sparse Core Ops, SparseCore 0:
  90.1 146.4 reduce-scatter.3
  332.7 51.8 reduce-scatter.5
  407.0 19.3 reduce-scatter.7
where the time goes:
time: 435 us; the launch traced here: 434 us
  waiting for transfers between devices  216 us (50%)
  blocking collectives  87.4 us (20%)
  local copies, waits for them, and re-layouts  49.2 us (11%)
  other arithmetic  44.1 us (10%)
  matrix products  14.2 us (3%)
  between operations  14.2 us (3%)
  starting transfers between devices  8.88 us (2%)
    reduce_scatter x1, waiting for transfers between devices, on_device(): lax.psum_scatter(partial_one, 'row', scatter_dimension=1, tiled=True)  144 us
    all_gather x1, blocking collectives, on_device(): group_one = lax.all_gather(coarse_one, 'row', axis=1, tiled=True)  72.1 us
    reduce_scatter x1, waiting for transfers between devices, on_device(): lax.psum_scatter(partial_two, 'col', scatter_dimension=1, tiled=True)  50.5 us
    scatter-add x3, other arithmetic, block_sums(): jax.ops.segment_sum(products, segment, num_segments=block_count + 1, indi...  27.3 us
    gather x3, local copies, waits for them, and re-layouts, add_points(): injected = jnp.take(own_piece, points, axis=1).astype(jnp.float32)  21 us
    reduce_scatter x1, waiting for transfers between devices, on_device(): lax.psum_scatter(partial_three, 'row', scatter_dimension=1, tiled=True)  17.8 us
    all_gather x1, blocking collectives, on_device(): group_two = lax.all_gather(coarse_two, 'col', axis=1, tiled=True)  15.3 us
    dot_general x1, matrix products, on_device(): jnp.einsum('sij,svj->svi', tiles_one, picked, preferred_element_type=jnp....  9.25 us
  transfers between devices with their start and end apart: 5, of which 4 were waited for; matrix products, arithmetic and copies ran while one was open for 6% of the time, Pallas kernels for 0%

commit v1 on v0

--- a/solution.py
+++ b/solution.py
@@ -83,7 +83,9 @@
     coarse_one = lax.psum_scatter(partial_one, "row", scatter_dimension=1, tiled=True).astype(
         jnp.bfloat16
     )
-    group_one = lax.all_gather(coarse_one, "row", axis=1, tiled=True)
+    group_one = jnp.concatenate(
+        lax.all_to_all(jnp.stack([coarse_one] * lax.axis_size("row")), "row", 0, 0), axis=1
+    )
     segment_second = slot_layout(pointers_two, tiles_two.shape[0])[1]
     partial_two = group_products(
         tiles_two, group_one, columns_two, segment_second, pointers_two.shape[0] - 1

time: 435 us -> 374 us (0.86)
  blocking collectives: 87.4 us -> 14.1 us
  waiting for transfers between devices: 216 us -> 227 us
    all_gather x1 -> x0, blocking collectives: 72.1 us -> none  [on_device(): group_one = lax.all_gather(coarse_one, 'row', axis=1, tiled=True)]
    all_to_all x0 -> x1, waiting for transfers between devices: none -> 11.1 us  [on_device(): lax.all_to_all(jnp.stack([coarse_one] * lax.axis_size('row')), 'row', 0, 0)]
    reshape x2 -> x1, local copies, waits for them, and re-layouts: 5.37 us -> 0.79 us  [group_products(): fine_group.reshape(vector_count, fine_group.shape[1] // tile_edge, tile_e...]
  transfers between devices with their start and end apart: 5 -> 6, of which waited for: 4 -> 5; matrix products, arithmetic and copies ran while one was open for 6% -> 8% of each run, Pallas kernels for 0% -> 0%
where the time goes in v1:
time: 374 us; the launch traced here: 373 us
  waiting for transfers between devices  227 us (61%)
  local copies, waits for them, and re-layouts  46.1 us (12%)
  other arithmetic  44.1 us (12%)
  matrix products  14.2 us (4%)
  between operations  14.2 us (4%)
  blocking collectives  14.1 us (4%)
  starting transfers between devices  13.1 us (4%)
    reduce_scatter x1, waiting for transfers between devices, on_device(): lax.psum_scatter(partial_one, 'row', scatter_dimension=1, tiled=True)  145 us
    reduce_scatter x1, waiting for transfers between devices, on_device(): lax.psum_scatter(partial_two, 'col', scatter_dimension=1, tiled=True)  48.9 us
    scatter-add x3, other arithmetic, block_sums(): jax.ops.segment_sum(products, segment, num_segments=block_count + 1, indi...  27.3 us
    gather x3, local copies, waits for them, and re-layouts, add_points(): injected = jnp.take(own_piece, points, axis=1).astype(jnp.float32)  21 us
    reduce_scatter x1, waiting for transfers between devices, on_device(): lax.psum_scatter(partial_three, 'row', scatter_dimension=1, tiled=True)  18.9 us
    all_gather x1, blocking collectives, on_device(): group_two = lax.all_gather(coarse_two, 'col', axis=1, tiled=True)  14.1 us
    all_to_all x1, waiting for transfers between devices, on_device(): lax.all_to_all(jnp.stack([coarse_one] * lax.axis_size('row')), 'row', 0, 0)  11.1 us
    dot_general x1, matrix products, on_device(): jnp.einsum('sij,svj->svi', tiles_one, picked, preferred_element_type=jnp....  9.25 us
  transfers between devices with their start and end apart: 6, of which 5 were waited for; matrix products, arithmetic and copies ran while one was open for 8% of the time, Pallas kernels for 0%

profile of v1, /device:TPU:0, one launch (start us, length us, event | category | flops | bytes accessed | tf_op | source)
XLA Modules:
  0.0 372.8 jit_solution(10182373773209408730)
XLA Ops:
  7.2 1.3 slice.33
  12.1 1.4 scatter_custom_fusion
  14.2 5.2 %all-to-all-start = ((s32[8,1,32]{2,1,0:T(1,128)}), s32[8,1,32]{2,1,0:T(1,128)S(1)}, u32[]{:S(2)}, u32[]{:S(2)}) async-start(s32[8,1,32]{2,1,0:T(1,128)} %all_to_all.16), calls=%async_computation | async-start | bytes 8192 | tf_op jit(solution)/shard_map/all_to_all | solution.py:75
  20.5 3.5 all-to-all-done
  26.2 3.6 all-to-all-start.1
  29.9 3.1 copy.81
  33.0 16.9 %gather_fusion.2 = bf16[4096,16]{1,0:T(8,128)(2,1)} fusion(bf16[16,16384]{0,1:T(8,128)(2,1)} %copy.81, s32[4096]{0:T(1024)S(1)} %fusion.16), kind=kCustom, calls=%fused_computation.2 | custom fusion | bytes 278528 | tf_op jit(solution)/shard_map/jit(_take)/gather | solution.py:34
  52.3 9.3 %fusion.1 = f32[256,16,128]{2,1,0:T(8,128)} fusion(bf16[256,128,128]{2,1,0:T(8,128)(2,1)} %param.14, bf16[256,16,128]{2,1,0:T(8,128)(2,1)S(1)} %gather_fusion.1, pred[256]{0:T(512)(128)(4,1)S(1)} %get-tuple-element.21), kind=kOutput, calls=%fused_computation.14 | convolution fusion | flops 134742016 | bytes 11534592 | tf_op jit(solution)/shard_map/sij,svj->svi/dot_general | solution.py:80
  61.6 20.6 %scatter_fusion = f32[129,16,128]{2,1,0:T(8,128)S(1)} fusion(f32[129,16,128]{2,1,0:T(8,128)S(1)} %broadcast_in_dim.121, s32[256]{0:T(256)S(1)} %bitcast.75, f32[256,16,128]{2,1,0:T(8,128)} %fusion.1), kind=kCustom, calls=%fused_computation.8 | custom fusion | flops 524288 | bytes 6292480 | tf_op jit(solution)/shard_map/scatter-add | solution.py:17
  82.3 4.6 %copy.98 = f32[16,128,128]{0,2,1:T(8,128)} copy(f32[16,128,128]{2,0,1:T(8,128)S(1)} %slice_bitcast_fusion) | data formatting | bytes 2097152 | tf_op jit(solution)/shard_map/reshape | solution.py:21
  87.0 3.0 fusion
  92.0 144.5 %reduce-scatter.4.cloned.1.call-done = f32[16,4096]{0,1:T(8,128)} async-done(((f32[16,16384]{0,1:T(8,128)}), f32[16,4096]{0,1:T(8,128)}) %reduce-scatter.4.cloned.1.call-update) | async-done | bytes 262160 | tf_op jit(solution)/shard_map/reduce_scatter | solution.py:83
  236.6 1.7 convert_element_type.35
  239.4 4.3 %all-to-all-start.2 = ((bf16[4,16,4096]{2,1,0:T(8,128)(2,1)}), bf16[4,16,4096]{2,1,0:T(8,128)(2,1)S(1)}, u32[]{:S(2)}, u32[]{:S(2)}) async-start(bf16[4,16,4096]{2,1,0:T(8,128)(2,1)} %stack.2), calls=%async_computation.3 | async-start | bytes 1048576 | tf_op jit(solution)/shard_map/all_to_all | solution.py:87
  243.8 3.2 gather_fusion.4
  247.0 11.1 %all-to-all-done.2 = bf16[4,16,4096]{2,1,0:T(8,128)(2,1)S(1)} async-done(((bf16[4,16,4096]{2,1,0:T(8,128)(2,1)}), bf16[4,16,4096]{2,1,0:T(8,128)(2,1)S(1)}, u32[]{:S(2)}, u32[]{:S(2)}) %all-to-all-start.2) | async-done | bytes 524320 | tf_op jit(solution)/shard_map/all_to_all | solution.py:87
  260.2 4.5 %fusion.5 = f32[128,16,128]{2,1,0:T(8,128)S(1)} fusion(bf16[128,128,128]{2,1,0:T(8,128)(2,1)} %param.18, bf16[128,16,128]{2,1,0:T(8,128)(2,1)S(1)} %gather_fusion.3, pred[128]{0:T(512)(128)(4,1)S(1)} %compare_and_fusion.5), kind=kOutput, calls=%fused_computation.22 | convolution fusion | flops 67371008 | bytes 5767296 | tf_op jit(solution)/shard_map/sij,vsj->svi/dot_general | solution.py:29
  264.7 5.5 %scatter_fusion.1 = f32[65,16,128]{2,1,0:T(8,128)S(1)} fusion(f32[65,16,128]{2,1,0:T(8,128)S(1)} %broadcast_in_dim.133, s32[128]{0:T(128)S(1)} %fusion.22, f32[128,16,128]{2,1,0:T(8,128)S(1)} %fusion.5), kind=kCustom, calls=%fused_computation.9 | custom fusion | flops 262144 | bytes 3146240 | tf_op jit(solution)/shard_map/scatter-add | solution.py:17
  270.3 2.6 copy.100
  272.9 2.0 fusion.4
  276.5 48.9 %reduce-scatter.6.cloned.1.call-done = f32[16,1024]{0,1:T(8,128)} async-done(((f32[16,8192]{0,1:T(8,128)}), f32[16,1024]{0,1:T(8,128)}) %reduce-scatter.6.cloned.1.call-update) | async-done | bytes 65552 | tf_op jit(solution)/shard_map/reduce_scatter | solution.py:94
  326.4 14.1 %all_gather.3 = bf16[16,8192]{0,1:T(8,128)(2,1)S(1)} all-gather(bf16[16,1024]{0,1:T(8,128)(2,1)S(1)} %convert_element_type.38), channel_id=1, replica_groups=mesh['row'=4,'col'=8] {'col'}, dimensions={1}, use_global_device_ids=true | all-gather | bytes 294912 | tf_op jit(solution)/shard_map/all_gather | solution.py:97
  346.1 18.9 %reduce-scatter.8.cloned.1.call-done = f32[16,256]{1,0:T(8,128)} async-done(((f32[16,1024]{1,0:T(8,128)}), f32[16,256]{1,0:T(8,128)}) %reduce-scatter.8.cloned.1.call-update) | async-done | bytes 16400 | tf_op jit(solution)/shard_map/reduce_scatter | solution.py:103
  365.0 1.3 convert_element_type.41
  (102 shorter events, 23.5 us)
Async XLA Ops:
  7.2 334.7 %copy-start = (bf16[16,128,128]{2,1,0:T(8,128)(2,1)S(1)}, bf16[16,128,128]{2,1,0:T(8,128)(2,1)}, u32[]{:S(2)}) copy-start(bf16[16,128,128]{2,1,0:T(8,128)(2,1)} %param.22) | copy-start | bytes 1572868
  7.2 22.7 %copy-start.8 = (s32[129]{0:T(256)S(1)}, s32[129]{0:T(256)}, u32[]{:S(2)}) copy-start(s32[129]{0:T(256)} %param.15) | copy-start | bytes 1552
  7.2 22.8 %copy-start.1 = (bf16[16,16384]{1,0:T(8,128)(2,1)S(1)}, bf16[16,16384]{1,0:T(8,128)(2,1)}, u32[]{:S(2)}) copy-start(bf16[16,16384]{1,0:T(8,128)(2,1)} %param.13) | copy-start | bytes 1572868
  7.2 22.6 %copy-start.5 = (s32[4096]{0:T(1024)S(1)}, s32[4096]{0:T(1024)}, u32[]{:S(2)}) copy-start(s32[4096]{0:T(1024)} %param.17) | copy-start | bytes 49156
  14.2 9.8 %all-to-all-start = ((s32[8,1,32]{2,1,0:T(1,128)}), s32[8,1,32]{2,1,0:T(1,128)S(1)}, u32[]{:S(2)}, u32[]{:S(2)}) async-start(s32[8,1,32]{2,1,0:T(1,128)} %all_to_all.16), calls=%async_computation | async-start | bytes 8192 | tf_op jit(solution)/shard_map/all_to_all | solution.py:75
  26.2 25.2 %all-to-all-start.1 = ((bf16[8,32,16,128]{3,2,1,0:T(8,128)(2,1)}), bf16[8,32,16,128]{3,2,1,0:T(8,128)(2,1)S(1)}, u32[]{:S(2)}, u32[]{:S(2)}) async-start(bf16[8,32,16,128]{3,2,1,0:T(8,128)(2,1)} %broadcast_select_fusion), calls=%async_computation.1 | async-start | bytes 2097152 | tf_op jit(solution)/shard_map/all_to_all | solution.py:77
  29.8 206.8 %reduce-scatter.4.cloned.1.call-start = ((), (), s32[]{:S(2)}) async-start(), calls=%async_computation.6 | async-start | bytes 10485760 | tf_op jit(solution)/shard_map/reduce_scatter | solution.py:83
  82.3 4.6 %copy-start.2 = (bf16[4096,16]{1,0:T(8,128)(2,1)S(1)}, bf16[4096,16]{1,0:T(8,128)(2,1)}, u32[]{:S(2)}) copy-start(bf16[4096,16]{1,0:T(8,128)(2,1)} %gather_fusion.2) | copy-start | bytes 393220
  89.9 0.7 copy-start.9
  89.9 1.4 copy-start.10
  89.9 1.4 copy-start.12
  90.6 153.2 %copy-start.7 = (s32[256]{0:T(256)S(1)}, s32[256]{0:T(256)}, u32[]{:S(2)}) copy-start(s32[256]{0:T(256)} %param.25) | copy-start | bytes 3076
  90.6 153.2 %copy-start.6 = (s32[1024]{0:T(1024)S(1)}, s32[1024]{0:T(1024)}, u32[]{:S(2)}) copy-start(s32[1024]{0:T(1024)} %param.21) | copy-start | bytes 12292
  238.6 26.1 %copy-start.3 = (bf16[16,4096]{1,0:T(8,128)(2,1)}, bf16[16,4096]{1,0:T(8,128)(2,1)S(1)}, u32[]{:S(2)}) copy-start(bf16[16,4096]{1,0:T(8,128)(2,1)S(1)} %copy.94) | copy-start | bytes 393220
  239.4 18.7 %all-to-all-start.2 = ((bf16[4,16,4096]{2,1,0:T(8,128)(2,1)}), bf16[4,16,4096]{2,1,0:T(8,128)(2,1)S(1)}, u32[]{:S(2)}, u32[]{:S(2)}) async-start(bf16[4,16,4096]{2,1,0:T(8,128)(2,1)} %stack.2), calls=%async_computation.3 | async-start | bytes 1048576 | tf_op jit(solution)/shard_map/all_to_all | solution.py:87
  243.7 81.6 %reduce-scatter.6.cloned.1.call-start = ((), (), s32[]{:S(2)}) async-start(), calls=%async_computation.7 | async-start | bytes 4718592 | tf_op jit(solution)/shard_map/reduce_scatter | solution.py:94
  270.3 4.7 %copy-start.11 = (s32[9]{0:T(128)S(1)}, s32[9]{0:T(128)}, u32[]{:S(2)}) copy-start(s32[9]{0:T(128)} %param.23) | copy-start | bytes 112
  275.0 90.0 %reduce-scatter.8.cloned.1.call-start = ((), (), s32[]{:S(2)}) async-start(), calls=%async_computation.8 | async-start | bytes 81920 | tf_op jit(solution)/shard_map/reduce_scatter | solution.py:103
  344.7 0.6 copy-start.4
Sparse Core Ops, SparseCore 0:
  90.1 146.4 reduce-scatter.3
  275.1 50.1 reduce-scatter.5
  345.5 19.4 reduce-scatter.7
